TPU v7x, 32 devices: a whole 2x2x4 slice. The times are simulated.
32 devices in a mesh: dp: 4 (over x, core), mp: 8 (over z, y).
Axes of the slice: x: 2, y: 2, z: 4, core: 2. Of those that a mesh axis runs over, the one named last changes fastest.
Arguments:
- tokens: bfloat16 [256, 8192], P('dp', 'mp'), may hold values from -80 to 80
- frozen_gate_weight: bfloat16 [8192, 28672], P('mp', 'dp'), may hold values from -0.198873782 to 0.198873782
- frozen_up_weight: bfloat16 [8192, 28672], P('mp', 'dp'), may hold values from -0.198873782 to 0.198873782
- frozen_down_weight: bfloat16 [28672, 8192], P('dp', 'mp'), may hold values from -0.28347335 to 0.28347335
- gate_left_factor: bfloat16 [8192, 16], P('mp'), may hold values from -0.0625 to 0.0625
- gate_right_factor: bfloat16 [16, 28672], P(None, 'dp'), may hold values from -0.75 to 0.75
- up_left_factor: bfloat16 [8192, 16], P('mp'), may hold values from -0.0625 to 0.0625
- up_right_factor: bfloat16 [16, 28672], P(None, 'dp'), may hold values from -0.75 to 0.75
- down_left_factor: bfloat16 [28672, 16], P('dp'), may hold values from -0.03125 to 0.03125
- down_right_factor: bfloat16 [16, 8192], P(None, 'mp'), may hold values from -0.75 to 0.75
- gate_column_magnitude: float32 [28672], P('dp'), may hold values from 0.5 to 2
- up_column_magnitude: float32 [28672], P('dp'), may hold values from 0.5 to 2
- down_column_magnitude: float32 [8192], P('mp'), may hold values from 0.5 to 2
- cotangent: bfloat16 [256, 8192], P('dp', 'mp'), may hold values from -80 to 80
Outputs:
- feedforward_output: bfloat16 [256, 8192], P('dp', 'mp')
- token_input_gradient: bfloat16 [256, 8192], P('dp', 'mp')
- gate_magnitude_gradient: float32 [28672], P('dp')
- up_magnitude_gradient: float32 [28672], P('dp')
- down_magnitude_gradient: float32 [8192], P('mp')
- gate_right_factor_gradient: float32 [16, 28672], P(None, 'dp')
- gate_left_factor_gradient: float32 [8192, 16], P('mp')
- up_right_factor_gradient: float32 [16, 28672], P(None, 'dp')
- up_left_factor_gradient: float32 [8192, 16], P('mp')
- down_right_factor_gradient: float32 [16, 8192], P(None, 'mp')
- down_left_factor_gradient: float32 [28672, 16], P('dp')
All inputs are finite; a program needn't handle non-finite values.
Results may differ from a plain program's by a relative error of at most 0.03.
Values may be sent and summed in bfloat16 or wider, within the bound.
No kernel may reach another device: no remote copies, remote signals or barrier semaphores. Data moves between devices by JAX's collectives and lax.ppermute only.
A program may use at most 192 MiB of HBM per device.

v0:
```python
import jax
import jax.numpy as jnp
from jax import lax
from jax.sharding import PartitionSpec as P

epsilon = 1e-06


def matrix_product(left_side, right_side):
    return jnp.dot(left_side, right_side, preferred_element_type=jnp.float32)


def matrix_product_right_transposed(left_side, right_side):
    return lax.dot_general(
        left_side, right_side, (((1,), (1,)), ((), ())), preferred_element_type=jnp.float32
    )


def matrix_product_left_transposed(left_side, right_side):
    return lax.dot_general(
        left_side, right_side, (((0,), (0,)), ((), ())), preferred_element_type=jnp.float32
    )


def combine_adapter_columns(weight_matrix, left_factor, right_factor):
    combined_weight = weight_matrix.astype(jnp.float32) + matrix_product(left_factor, right_factor)
    return (
        combined_weight.astype(jnp.bfloat16),
        jnp.sum(combined_weight * combined_weight, axis=0),
    )


def activate(pre_pair, scale_gate, scale_up):
    width = scale_gate.shape[0]
    pre_gate = pre_pair[:, :width]
    pre_up = pre_pair[:, width:]
    gate_act = pre_gate * scale_gate
    up_act = pre_up * scale_up
    sigmoid_gate = jax.nn.sigmoid(gate_act)
    silu_gate = gate_act * sigmoid_gate
    hidden_state = (silu_gate * up_act).astype(jnp.bfloat16)
    return (hidden_state, (pre_gate, pre_up, gate_act, up_act, sigmoid_gate, silu_gate))


def gate_backward(grad_hidden, saved, scale_gate, scale_up):
    pre_gate, pre_up, gate_act, up_act, sigmoid_gate, silu_gate = saved
    grad_gate = grad_hidden * up_act * sigmoid_gate * (1.0 + gate_act * (1.0 - sigmoid_gate))
    grad_up = grad_hidden * silu_gate
    gate_logits = (grad_gate * scale_gate).astype(jnp.bfloat16)
    up_logits = (grad_up * scale_up).astype(jnp.bfloat16)
    return (
        gate_logits,
        up_logits,
        jnp.sum(grad_gate * pre_gate, axis=0),
        jnp.sum(grad_up * pre_up, axis=0),
    )


def per_device(
    tokens,
    frozen_gate_weight,
    frozen_up_weight,
    frozen_down_weight,
    gate_left_factor,
    gate_right_factor,
    up_left_factor,
    up_right_factor,
    down_left_factor,
    down_right_factor,
    gate_column_magnitude,
    up_column_magnitude,
    down_column_magnitude,
    cotangent,
):
    combined_gate_weight, gate_squared_columns = combine_adapter_columns(
        frozen_gate_weight, gate_left_factor, gate_right_factor
    )
    combined_up_weight, up_squared_columns = combine_adapter_columns(
        frozen_up_weight, up_left_factor, up_right_factor
    )
    combined_down_weight, down_squared_columns = combine_adapter_columns(
        frozen_down_weight, down_left_factor, down_right_factor
    )
    gate_squared_columns, up_squared_columns = lax.psum(
        (gate_squared_columns, up_squared_columns), "mp"
    )
    down_squared_columns = lax.psum(down_squared_columns, "dp")
    gate_column_norm = jnp.sqrt(gate_squared_columns + epsilon)
    up_column_norm = jnp.sqrt(up_squared_columns + epsilon)
    down_column_norm = jnp.sqrt(down_squared_columns + epsilon)
    scale_gate = gate_column_magnitude / gate_column_norm
    scale_up = up_column_magnitude / up_column_norm
    scale_down = down_column_magnitude / down_column_norm
    collected_rows = lax.all_gather(tokens, "dp", axis=0, tiled=True)
    local_rows = collected_rows.shape[0] // lax.axis_size("mp")
    row_start = lax.axis_index("mp") * local_rows
    gate_projection_output, up_projection_output = (
        lax.psum(
            matrix_product(collected_rows, gate_left_factor).astype(jnp.bfloat16), "mp"
        ).astype(jnp.float32),
        lax.psum(matrix_product(collected_rows, up_left_factor).astype(jnp.bfloat16), "mp").astype(
            jnp.float32
        ),
    )
    gate_projection_output = gate_projection_output.astype(jnp.bfloat16)
    up_projection_output = up_projection_output.astype(jnp.bfloat16)
    row_block = collected_rows
    pre_pair = lax.psum_scatter(
        jnp.concatenate(
            [
                matrix_product(row_block, combined_gate_weight),
                matrix_product(row_block, combined_up_weight),
            ],
            axis=1,
        ).astype(jnp.bfloat16),
        "mp",
        scatter_dimension=0,
        tiled=True,
    ).astype(jnp.float32)
    hidden_local, saved = activate(pre_pair, scale_gate, scale_up)
    hidden_state_full = lax.all_gather(hidden_local, "mp", axis=0, tiled=True)
    row_block = hidden_state_full
    down_preactivation = lax.psum_scatter(
        matrix_product(row_block, combined_down_weight).astype(jnp.bfloat16),
        "dp",
        scatter_dimension=0,
        tiled=True,
    ).astype(jnp.float32)
    feedforward_output = (down_preactivation * scale_down).astype(jnp.bfloat16)
    output_cotangent = cotangent.astype(jnp.float32)
    down_logits = (output_cotangent * scale_down).astype(jnp.bfloat16)
    down_projection_output, mag_down_sum = (
        lax.psum(
            matrix_product(hidden_state_full, down_left_factor).astype(jnp.bfloat16), "dp"
        ).astype(jnp.float32),
        lax.psum(
            jnp.sum(output_cotangent * down_preactivation, axis=0).astype(jnp.bfloat16), "dp"
        ).astype(jnp.float32),
    )
    down_projection_output = down_projection_output.astype(jnp.bfloat16)
    down_magnitude_gradient = mag_down_sum / down_column_norm
    down_logits_full = lax.all_gather(down_logits, "dp", axis=0, tiled=True)
    down_backward_rows = lax.psum(
        matrix_product_right_transposed(down_logits_full, down_right_factor).astype(jnp.bfloat16),
        "mp",
    )
    down_right_factor_gradient = matrix_product_left_transposed(
        down_projection_output, down_logits_full
    )
    down_left_factor_gradient = matrix_product_left_transposed(
        hidden_state_full, down_backward_rows
    )
    row_block = down_logits_full
    grad_hidden = lax.psum_scatter(
        matrix_product_right_transposed(row_block, combined_down_weight).astype(jnp.bfloat16),
        "mp",
        scatter_dimension=0,
        tiled=True,
    ).astype(jnp.float32)
    gate_logits, up_logits, mag_gate_terms, mag_up_terms = gate_backward(
        grad_hidden, saved, scale_gate, scale_up
    )
    proj_gate_rows = lax.dynamic_slice_in_dim(gate_projection_output, row_start, local_rows, 0)
    proj_up_rows = lax.dynamic_slice_in_dim(up_projection_output, row_start, local_rows, 0)
    gate_backward_rows, up_backward_rows = lax.psum(
        (
            matrix_product_right_transposed(gate_logits, gate_right_factor),
            matrix_product_right_transposed(up_logits, up_right_factor),
        ),
        "dp",
    )
    gate_backward_rows, up_backward_rows = (
        lax.all_gather(gate_backward_rows.astype(jnp.bfloat16), "mp", axis=0, tiled=True),
        lax.all_gather(up_backward_rows.astype(jnp.bfloat16), "mp", axis=0, tiled=True),
    )
    (
        gate_magnitude_total,
        up_magnitude_total,
        gate_right_factor_gradient,
        up_right_factor_gradient,
    ) = (
        lax.psum(mag_gate_terms.astype(jnp.bfloat16), "mp").astype(jnp.float32),
        lax.psum(mag_up_terms.astype(jnp.bfloat16), "mp").astype(jnp.float32),
        lax.psum(
            matrix_product_left_transposed(proj_gate_rows, gate_logits).astype(jnp.bfloat16), "mp"
        ).astype(jnp.float32),
        lax.psum(
            matrix_product_left_transposed(proj_up_rows, up_logits).astype(jnp.bfloat16), "mp"
        ).astype(jnp.float32),
    )
    z_gate_full, z_up_full = (
        lax.all_gather(gate_logits, "mp", axis=0, tiled=True),
        lax.all_gather(up_logits, "mp", axis=0, tiled=True),
    )
    gate_magnitude_gradient = gate_magnitude_total / gate_column_norm
    up_magnitude_gradient = up_magnitude_total / up_column_norm
    gate_left_factor_gradient = matrix_product_left_transposed(collected_rows, gate_backward_rows)
    up_left_factor_gradient = matrix_product_left_transposed(collected_rows, up_backward_rows)
    token_input_gradient = lax.psum_scatter(
        (
            matrix_product_right_transposed(z_gate_full, combined_gate_weight)
            + matrix_product_right_transposed(z_up_full, combined_up_weight)
        ).astype(jnp.bfloat16),
        "dp",
        scatter_dimension=0,
        tiled=True,
    )
    return (
        feedforward_output,
        token_input_gradient,
        gate_magnitude_gradient,
        up_magnitude_gradient,
        down_magnitude_gradient,
        gate_right_factor_gradient,
        gate_left_factor_gradient,
        up_right_factor_gradient,
        up_left_factor_gradient,
        down_right_factor_gradient,
        down_left_factor_gradient,
    )


def solution(mesh):
    placed = (
        P("dp", "mp"),
        P("mp", "dp"),
        P("mp", "dp"),
        P("dp", "mp"),
        P("mp", None),
        P(None, "dp"),
        P("mp", None),
        P(None, "dp"),
        P("dp", None),
        P(None, "mp"),
        P("dp"),
        P("dp"),
        P("mp"),
        P("dp", "mp"),
    )
    return jax.shard_map(
        per_device,
        mesh=mesh,
        in_specs=placed,
        out_specs=(
            P("dp", "mp"),
            P("dp", "mp"),
            P("dp"),
            P("dp"),
            P("mp"),
            P(None, "dp"),
            P("mp", None),
            P(None, "dp"),
            P("mp", None),
            P(None, "mp"),
            P("dp", None),
        ),
        check_vma=False,
    )
```

profile of v0, /device:TPU:0, one launch (start us, length us, event | category | flops | bytes accessed | tf_op | source)
XLA Modules:
  0.0 689.3 jit_solution(208738933042338539)
XLA Ops:
  7.2 9.0 %all_gather.21 = bf16[256,1024]{1,0:T(8,128)(2,1)S(1)} all-gather(bf16[64,1024]{1,0:T(8,128)(2,1)} %param.14), channel_id=1, replica_groups=mesh['dp'=4,'mp'=8] {'dp'}, dimensions={0}, use_global_device_ids=true | all-gather | bytes 655360 | tf_op jit(solution)/shard_map/all_gather | solution.py:94
  16.2 15.0 %multiply_reduce_fusion.1 = (f32[7168]{0:T(1024)S(1)}, f32[1024,7168]{1,0:T(8,128)}) fusion(bf16[1024,7168]{1,0:T(8,128)(2,1)} %param.16, bf16[1024,16]{0,1:T(8,128)(2,1)} %param.20, bf16[16,7168]{1,0:T(8,128)(2,1)} %param.21), kind=kOutput, calls=%fused_computation.2 | convolution fusion | flops 264233984 | bytes 44331008 | tf_op jit(solution)/shard_map/dot_general | solution.py:10
  31.2 18.4 %fusion.4 = bf16[256,7168]{0,1:T(8,128)(2,1)} fusion(bf16[256,1024]{1,0:T(8,128)(2,1)S(1)} %all_gather.21, f32[1024,7168]{1,0:T(8,128)} %get-tuple-element.34, bf16[1024,7168]{1,0:T(8,128)(2,1)} %param.16), kind=kOutput, calls=%fused_computation.13 | convolution fusion | flops 3781951488 | bytes 48234496 | tf_op jit(solution)/shard_map/dot_general | solution.py:10
  49.6 14.7 %multiply_reduce_fusion.2 = (f32[7168]{0:T(1024)S(1)}, f32[1024,7168]{1,0:T(8,128)}) fusion(bf16[1024,7168]{1,0:T(8,128)(2,1)} %param.15, bf16[1024,16]{0,1:T(8,128)(2,1)S(1)} %copy-done.6, bf16[16,7168]{1,0:T(8,128)(2,1)S(1)} %copy-done), kind=kOutput, calls=%fused_computation.3 | convolution fusion | flops 264233984 | bytes 44331008 | tf_op jit(solution)/shard_map/dot_general | solution.py:10
  64.4 18.4 %fusion.3 = bf16[256,7168]{0,1:T(8,128)(2,1)} fusion(bf16[256,1024]{1,0:T(8,128)(2,1)S(1)} %all_gather.21, f32[1024,7168]{1,0:T(8,128)} %get-tuple-element.36, bf16[1024,7168]{1,0:T(8,128)(2,1)} %param.15), kind=kOutput, calls=%fused_computation.12 | convolution fusion | flops 3781951488 | bytes 48234496 | tf_op jit(solution)/shard_map/dot_general | solution.py:10
  82.7 8.8 %pad_maximum_fusion = bf16[256,14336]{0,1:T(8,128)(2,1)} fusion(bf16[256,7168]{0,1:T(8,128)(2,1)} %fusion.4, bf16[256,7168]{0,1:T(8,128)(2,1)} %fusion.3), kind=kLoop, calls=%fused_computation.16 | loop fusion | flops 14680064 | bytes 14680064 | tf_op jit(solution)/shard_map/concatenate | solution.py:109
  91.5 10.2 %copy.40 = bf16[256,14336]{1,0:T(8,128)(2,1)} copy(bf16[256,14336]{0,1:T(8,128)(2,1)} %pad_maximum_fusion) | data formatting | bytes 14680064
  101.9 15.4 %multiply_reduce_fusion = (f32[1024]{0:T(1024)S(1)}, f32[7168,1024]{1,0:T(8,128)}) fusion(bf16[7168,1024]{1,0:T(8,128)(2,1)} %param.17, bf16[7168,16]{0,1:T(8,128)(2,1)S(1)} %copy-done.3, bf16[16,1024]{1,0:T(8,128)(2,1)S(1)} %copy-done.8), kind=kOutput, calls=%fused_computation | convolution fusion | flops 264240128 | bytes 44306432 | tf_op jit(solution)/shard_map/dot_general | solution.py:10
  117.2 7.1 %psum.100 = f32[1024]{0:T(1024)S(1)} all-reduce(f32[1024]{0:T(1024)S(1)} %get-tuple-element.31), channel_id=1, replica_groups=mesh['dp'=4,'mp'=8] {'dp'}, use_global_device_ids=true, to_apply=%region_7.0 | all-reduce | flops 1024 | bytes 8192 | tf_op jit(solution)/shard_map/psum | solution.py:87
  124.4 6.6 all_gather.23
  131.0 18.8 %convolution_convert_fusion.2 = bf16[256,7168]{1,0:T(8,128)(2,1)} fusion(bf16[256,1024]{1,0:T(8,128)(2,1)S(1)} %all_gather.23, f32[7168,1024]{1,0:T(8,128)} %get-tuple-element.32, bf16[7168,1024]{1,0:T(8,128)(2,1)} %param.17), kind=kOutput, calls=%fused_computation.11 | convolution fusion | flops 3781951488 | bytes 48234496 | tf_op jit(solution)/shard_map/dot_general | solution.py:14
  149.9 39.8 %all-reduce = (f32[7168]{0:T(1024)S(1)}, f32[7168]{0:T(1024)S(1)}) all-reduce(f32[7168]{0:T(1024)S(1)} %get-tuple-element.33, f32[7168]{0:T(1024)S(1)} %get-tuple-element.35), channel_id=1, replica_groups=mesh['dp'=4,'mp'=8] {'mp'}, use_global_device_ids=true, to_apply=%region_4.0 | all-reduce | flops 14336 | bytes 114688 | tf_op jit(solution)/shard_map/psum | solution.py:84
  190.6 47.0 %reduce-scatter.13.cloned.1.call-done = bf16[32,14336]{1,0:T(8,128)(2,1)} async-done(((bf16[256,14336]{1,0:T(8,128)(2,1)}), bf16[32,14336]{1,0:T(8,128)(2,1)}) %reduce-scatter.13.cloned.1.call-update) | async-done | bytes 917520 | tf_op jit(solution)/shard_map/reduce_scatter | solution.py:108
  237.5 2.6 convert_element_type.113
  240.1 81.1 %reduce-scatter.15.cloned.1.call-done = bf16[32,7168]{1,0:T(8,128)(2,1)} async-done(((bf16[256,7168]{1,0:T(8,128)(2,1)}), bf16[32,7168]{1,0:T(8,128)(2,1)}) %reduce-scatter.15.cloned.1.call-update) | async-done | bytes 458768 | tf_op jit(solution)/shard_map/reduce_scatter | solution.py:154
  321.2 3.0 multiply_reduce_fusion.3
  324.4 36.5 %all-reduce.2 = (bf16[7168]{0:T(1024)(128)(2,1)S(1)}, bf16[7168]{0:T(1024)(128)(2,1)S(1)}, bf16[256,16]{0,1:T(8,128)(2,1)S(1)}, bf16[256,16]{0,1:T(8,128)(2,1)S(1)}, bf16[256,16]{0,1:T(8,128)(2,1)S(1)}) all-reduce(bf16[7168]{0:T(1024)(128)(2,1)S(1)} %get-tuple-element.12, ...), channel_id=1, replica_groups=mesh['dp'=4,'mp'=8] {'mp'}, use_global_device_ids=true, to_apply=%region_11.0 | all-reduce | flops 26624 | bytes 106496 | tf_op jit(solution)/shard_map/psum | solution.py:182
  367.2 10.2 %all-reduce.1 = (bf16[32,16]{0,1:T(8,128)(2,1)S(1)}, bf16[32,16]{0,1:T(8,128)(2,1)S(1)}) all-reduce(f32[32,16]{0,1:T(8,128)S(1)} %fusion.27, f32[32,16]{0,1:T(8,128)S(1)} %fusion.28), channel_id=1, replica_groups=mesh['dp'=4,'mp'=8] {'dp'}, use_global_device_ids=true, to_apply=%region_18.0 | all-reduce | flops 1024 | bytes 6144 | tf_op jit(solution)/shard_map/psum | solution.py:165
  377.3 30.6 %all-gather = bf16[8,32,16]{1,2,0:T(8,128)(2,1)S(1)} all-gather(bf16[1,32,16]{1,2,0:T(8,128)(2,1)S(1)} %bitcast.55), channel_id=1, replica_groups=mesh['dp'=4,'mp'=8] {'mp'}, dimensions={0}, use_global_device_ids=true | all-gather | bytes 9216 | tf_op jit(solution)/shard_map/all_gather | solution.py:173
  408.0 30.6 %all-gather.1 = bf16[8,32,16]{1,2,0:T(8,128)(2,1)S(1)} all-gather(bf16[1,32,16]{1,2,0:T(8,128)(2,1)S(1)} %bitcast.54), channel_id=1, replica_groups=mesh['dp'=4,'mp'=8] {'mp'}, dimensions={0}, use_global_device_ids=true | all-gather | bytes 9216 | tf_op jit(solution)/shard_map/all_gather | solution.py:174
  441.0 1.8 convert_element_type.135
  442.8 1.7 convert_element_type.139
  444.5 56.3 %all-gather.6.cloned.1.call-done = bf16[256,7168]{1,0:T(8,128)(2,1)} async-done(((bf16[32,7168]{1,0:T(8,128)(2,1)}), bf16[256,7168]{1,0:T(8,128)(2,1)}) %all-gather.6.cloned.1.call-update) | async-done | bytes 3670032 | tf_op jit(solution)/shard_map/all_gather | solution.py:121
  500.9 18.0 %convolution_convert_fusion.5 = bf16[256,1024]{1,0:T(8,128)(2,1)} fusion(bf16[256,7168]{1,0:T(8,128)(2,1)} %all-gather.6.cloned.1.call-done, f32[7168,1024]{1,0:T(8,128)} %get-tuple-element.32, bf16[7168,1024]{1,0:T(8,128)(2,1)} %param.17), kind=kOutput, calls=%fused_computation.19 | convolution fusion | flops 3780378624 | bytes 48234496 | tf_op jit(solution)/shard_map/dot_general | solution.py:10
  518.9 48.9 %all-gather.8.cloned.1.call-done = bf16[256,7168]{1,0:T(8,128)(2,1)} async-done(((bf16[32,7168]{1,0:T(8,128)(2,1)}), bf16[256,7168]{1,0:T(8,128)(2,1)}) %all-gather.8.cloned.1.call-update) | async-done | bytes 3670032 | tf_op jit(solution)/shard_map/all_gather | solution.py:192
  567.9 16.5 %fusion.23 = f32[256,1024]{1,0:T(8,128)S(1)} fusion(bf16[256,7168]{1,0:T(8,128)(2,1)} %all-gather.8.cloned.1.call-done, f32[1024,7168]{1,0:T(8,128)} %get-tuple-element.36, bf16[1024,7168]{1,0:T(8,128)(2,1)} %param.15), kind=kOutput, calls=%fused_computation.60 | convolution fusion | flops 3780116480 | bytes 48758784 | tf_op jit(solution)/shard_map/dot_general | solution.py:14
  584.4 50.5 %all-gather.10.cloned.1.call-done = bf16[256,7168]{1,0:T(8,128)(2,1)} async-done(((bf16[32,7168]{1,0:T(8,128)(2,1)}), bf16[256,7168]{1,0:T(8,128)(2,1)}) %all-gather.10.cloned.1.call-update) | async-done | bytes 3670032 | tf_op jit(solution)/shard_map/all_gather | solution.py:193
  634.9 17.6 %fusion.5 = bf16[256,1024]{1,0:T(8,128)(2,1)} fusion(f32[256,1024]{1,0:T(8,128)S(1)} %fusion.23, bf16[256,7168]{1,0:T(8,128)(2,1)} %all-gather.10.cloned.1.call-done, f32[1024,7168]{1,0:T(8,128)} %get-tuple-element.34, bf16[1024,7168]{1,0:T(8,128)(2,1)} %param.16), kind=kOutput, calls=%fused_computation.18 | convolution fusion | flops 3780640768 | bytes 49283072 | tf_op jit(solution)/shard_map/dot_general | solution.py:14
  652.5 3.1 convolution_convert_fusion.6
  655.6 3.5 fusion.30
  660.6 10.1 %all-reduce.4 = (bf16[1024]{0:T(1024)(128)(2,1)S(1)}, bf16[256,16]{0,1:T(8,128)(2,1)S(1)}) all-reduce(bf16[1024]{0:T(1024)(128)(2,1)S(1)} %get-tuple-element.29, bf16[256,16]{0,1:T(8,128)(2,1)S(1)} %convolution_convert_fusion.6), channel_id=1, replica_groups=mesh['dp'=4,'mp'=8] {'dp'}, use_global_device_ids=true, to_apply=%region_15.0 | all-reduce | flops 5120 | bytes 20480 | tf_op jit(solution)/shard_map/psum | solution.py:136
  672.2 10.3 %reduce-scatter.11.cloned.1.call-done = bf16[64,1024]{1,0:T(8,128)(2,1)} async-done(((bf16[256,1024]{1,0:T(8,128)(2,1)}), bf16[64,1024]{1,0:T(8,128)(2,1)}) %reduce-scatter.11.cloned.1.call-update) | async-done | bytes 131088 | tf_op jit(solution)/shard_map/reduce_scatter | solution.py:199
  (64 shorter events, 12.9 us)
Async XLA Ops:
  7.2 42.5 %copy-start = (bf16[16,7168]{1,0:T(8,128)(2,1)S(1)}, bf16[16,7168]{1,0:T(8,128)(2,1)}, u32[]{:S(2)}) copy-start(bf16[16,7168]{1,0:T(8,128)(2,1)} %param.19) | copy-start | bytes 688132
  7.2 230.3 %reduce-scatter.13.cloned.1.call-start = ((), (), s32[]{:S(2)}) async-start(), calls=%async_computation.9 | async-start | bytes 8257536 | tf_op jit(solution)/shard_map/reduce_scatter | solution.py:108
  31.2 18.4 %copy-start.6 = (bf16[1024,16]{0,1:T(8,128)(2,1)S(1)}, bf16[1024,16]{0,1:T(8,128)(2,1)}, u32[]{:S(2)}) copy-start(bf16[1024,16]{0,1:T(8,128)(2,1)} %param.18) | copy-start | bytes 98308
  91.5 10.3 %copy-start.3 = (bf16[7168,16]{0,1:T(8,128)(2,1)S(1)}, bf16[7168,16]{0,1:T(8,128)(2,1)}, u32[]{:S(2)}) copy-start(bf16[7168,16]{0,1:T(8,128)(2,1)} %param.22) | copy-start | bytes 688132
  91.5 10.3 %copy-start.8 = (bf16[16,1024]{1,0:T(8,128)(2,1)S(1)}, bf16[16,1024]{1,0:T(8,128)(2,1)}, u32[]{:S(2)}) copy-start(bf16[16,1024]{1,0:T(8,128)(2,1)} %param.23) | copy-start | bytes 98308
  101.8 22.6 %copy-start.11 = (f32[1024]{0:T(1024)S(1)}, f32[1024]{0:T(1024)}, u32[]{:S(2)}) copy-start(f32[1024]{0:T(1024)} %param.26) | copy-start | bytes 12292
  101.8 22.6 %copy-start.5 = (bf16[64,1024]{1,0:T(8,128)(2,1)S(1)}, bf16[64,1024]{1,0:T(8,128)(2,1)}, u32[]{:S(2)}) copy-start(bf16[64,1024]{1,0:T(8,128)(2,1)} %param.27) | copy-start | bytes 393220
  101.8 219.4 %reduce-scatter.15.cloned.1.call-start = ((), (), s32[]{:S(2)}) async-start(), calls=%async_computation.10 | async-start | bytes 4128768 | tf_op jit(solution)/shard_map/reduce_scatter | solution.py:154
  131.0 58.7 %copy-start.9 = (f32[7168]{0:T(1024)S(1)}, f32[7168]{0:T(1024)}, u32[]{:S(2)}) copy-start(f32[7168]{0:T(1024)} %param.24) | copy-start | bytes 86020
  131.0 58.8 %copy-start.10 = (f32[7168]{0:T(1024)S(1)}, f32[7168]{0:T(1024)}, u32[]{:S(2)}) copy-start(f32[7168]{0:T(1024)} %param.25) | copy-start | bytes 86020
  131.0 59.0 %copy-start.7 = (bf16[1024,16]{0,1:T(8,128)(2,1)S(1)}, bf16[1024,16]{0,1:T(8,128)(2,1)}, u32[]{:S(2)}) copy-start(bf16[1024,16]{0,1:T(8,128)(2,1)} %param.20) | copy-start | bytes 98308
  149.9 216.0 %copy-start.4 = (bf16[16,7168]{1,0:T(8,128)(2,1)S(1)}, bf16[16,7168]{1,0:T(8,128)(2,1)}, u32[]{:S(2)}) copy-start(bf16[16,7168]{1,0:T(8,128)(2,1)} %param.21) | copy-start | bytes 688132
  149.9 291.1 %all-reduce.7.cloned.1.call-start = ((), (), s32[]{:S(2)}) async-start(), calls=%async_computation.11 | async-start | bytes 917504 | tf_op jit(solution)/shard_map/psum | solution.py:184
  324.3 39.8 %copy-start.1 = (bf16[32,7168]{1,0:T(8,128)(2,1)}, bf16[32,7168]{1,0:T(8,128)(2,1)S(1)}, u32[]{:S(2)}) copy-start(bf16[32,7168]{1,0:T(8,128)(2,1)S(1)} %get-tuple-element.27) | copy-start | bytes 1376260
  324.3 39.1 %copy-start.2 = (bf16[32,7168]{1,0:T(8,128)(2,1)}, bf16[32,7168]{1,0:T(8,128)(2,1)S(1)}, u32[]{:S(2)}) copy-start(bf16[32,7168]{1,0:T(8,128)(2,1)S(1)} %multiply_convert_fusion.1) | copy-start | bytes 1376260
  362.8 138.0 %all-gather.6.cloned.1.call-start = ((), (), s32[]{:S(2)}) async-start(), calls=%async_computation.4 | async-start | bytes 4128768 | tf_op jit(solution)/shard_map/all_gather | solution.py:121
  363.4 204.4 %all-gather.8.cloned.1.call-start = ((), (), s32[]{:S(2)}) async-start(), calls=%async_computation.6 | async-start | bytes 4128768 | tf_op jit(solution)/shard_map/all_gather | solution.py:192
  364.0 270.8 %all-gather.10.cloned.1.call-start = ((), (), s32[]{:S(2)}) async-start(), calls=%async_computation.7 | async-start | bytes 4128768 | tf_op jit(solution)/shard_map/all_gather | solution.py:193
  364.6 294.4 %reduce-scatter.9.cloned.1.call-start = ((), (), s32[]{:S(2)}) async-start(), calls=%async_computation.5 | async-start | bytes 655360 | tf_op jit(solution)/shard_map/reduce_scatter | solution.py:123
  518.9 163.6 %reduce-scatter.11.cloned.1.call-start = ((), (), s32[]{:S(2)}) async-start(), calls=%async_computation.8 | async-start | bytes 655360 | tf_op jit(solution)/shard_map/reduce_scatter | solution.py:199
Sparse Core Ops, SparseCore 0:
  101.9 135.5 reduce-scatter.12
  241.2 80.0 reduce-scatter.14
  363.0 69.7 all-reduce.6
  435.3 65.4 all-gather.5
  502.9 64.9 all-gather.7
  569.9 64.9 all-gather.9
  637.3 20.3 reduce-scatter.8
  660.8 21.6 reduce-scatter.10
where the time goes:
time: 690 us; the launch traced here: 689 us
  waiting for transfers between devices  296 us (43%)
  blocking collectives  181 us (26%)
  matrix products  167 us (24%)
  other arithmetic  20.9 us (3%)
  between operations  14.3 us (2%)
  local copies, waits for them, and re-layouts  10.5 us (2%)
    dot_general x9, matrix products, matrix_product(): return jnp.dot(left_side, right_side, preferred_element_type=jnp.float32)  103 us
    reduce_scatter x1, waiting for transfers between devices, per_device(): lax.psum_scatter(matrix_product_right_transposed(row_block, combined_down...  81.1 us
    all_gather x1, waiting for transfers between devices, per_device(): hidden_state_full = lax.all_gather(hidden_local, 'mp', axis=0, tiled=True)  56.3 us
    dot_general x6, matrix products, matrix_product_right_transposed(): lax.dot_general(left_side, right_side, (((1,), (1,)), ((), ())), preferre...  55.7 us
    all_gather x1, waiting for transfers between devices, per_device(): lax.all_gather(up_logits, 'mp', axis=0, tiled=True)  50.5 us
    all_gather x1, waiting for transfers between devices, per_device(): lax.all_gather(gate_logits, 'mp', axis=0, tiled=True)  48.9 us
    reduce_scatter x1, waiting for transfers between devices, per_device(): lax.psum_scatter(jnp.concatenate([matrix_product(row_block, combined_gate...  47 us
    psum x1, blocking collectives, per_device(): lax.psum((gate_squared_columns, up_squared_columns), 'mp')  39.8 us
  transfers between devices with their start and end apart: 8, of which 6 were waited for; matrix products, arithmetic and copies ran while one was open for 16% of the time, Pallas kernels for 0%

commit v1 on v0

--- a/solution.py
+++ b/solution.py
@@ -118,7 +118,20 @@
         tiled=True,
     ).astype(jnp.float32)
     hidden_local, saved = activate(pre_pair, scale_gate, scale_up)
-    hidden_state_full = lax.all_gather(hidden_local, "mp", axis=0, tiled=True)
+
+    def find_terms_now(matrix, peer_axis):
+        slots = lax.psum(1, peer_axis)
+        blocks_here = [matrix]
+        for tick in tuple(range(slots - 1)):
+            reached = lax.ppermute(
+                blocks_here[-1], peer_axis, [(k0, (k0 + 1) % slots) for k0 in range(slots)]
+            )
+            blocks_here.append(reached)
+        prior = jnp.concatenate(blocks_here[::-1], axis=0)
+        frame_out = lax.axis_index(peer_axis)
+        return jnp.roll(prior, (frame_out + 1) * matrix.shape[0], axis=0)
+
+    hidden_state_full = find_terms_now(hidden_local, "mp")
     row_block = hidden_state_full
     down_preactivation = lax.psum_scatter(
         matrix_product(row_block, combined_down_weight).astype(jnp.bfloat16),

time: 690 us -> 651 us (0.943)
  waiting for transfers between devices: 296 us -> 227 us
  local copies, waits for them, and re-layouts: 10.5 us -> 33.8 us
    ppermute x0 -> x7, waiting for transfers between devices: none -> 99.2 us  [find_terms_now(): lax.ppermute(blocks_here[-1], peer_axis, [(k0, (k0 + 1) % slots) for k0 i...]
    all_gather x1 -> x0, waiting for transfers between devices: 56.3 us -> none  [per_device(): hidden_state_full = lax.all_gather(hidden_local, 'mp', axis=0, tiled=True)]
    all_gather x1, waiting for transfers between devices: 50.5 us -> 0.02 us  [per_device(): lax.all_gather(up_logits, 'mp', axis=0, tiled=True)]
    all_gather x1, waiting for transfers between devices: 48.9 us -> 0.02 us  [per_device(): lax.all_gather(gate_logits, 'mp', axis=0, tiled=True)]
    unnamed x27 -> x48, local copies, waits for them, and re-layouts: 10.5 us -> 33 us
    reduce_scatter x1, waiting for transfers between devices: 10.3 us -> 0.01 us  [per_device(): lax.psum_scatter((matrix_product_right_transposed(z_gate_full, combined_g...]
  transfers between devices with their start and end apart: 8 -> 14, of which waited for: 6 -> 8; matrix products, arithmetic and copies ran while one was open for 16% -> 20% of each run, Pallas kernels for 0% -> 0%
where the time goes in v1:
time: 651 us; the launch traced here: 649 us
  waiting for transfers between devices  227 us (35%)
  blocking collectives  183 us (28%)
  matrix products  167 us (26%)
  local copies, waits for them, and re-layouts  33.8 us (5%)
  other arithmetic  20.9 us (3%)
  between operations  14.4 us (2%)
    dot_general x9, matrix products, matrix_product(): return jnp.dot(left_side, right_side, preferred_element_type=jnp.float32)  103 us
    ppermute x7, waiting for transfers between devices, find_terms_now(): lax.ppermute(blocks_here[-1], peer_axis, [(k0, (k0 + 1) % slots) for k0 i...  99.2 us
    reduce_scatter x1, waiting for transfers between devices, per_device(): lax.psum_scatter(matrix_product_right_transposed(row_block, combined_down...  81.1 us
    dot_general x6, matrix products, matrix_product_right_transposed(): lax.dot_general(left_side, right_side, (((1,), (1,)), ((), ())), preferre...  55.9 us
    reduce_scatter x1, waiting for transfers between devices, per_device(): lax.psum_scatter(jnp.concatenate([matrix_product(row_block, combined_gate...  46 us
    psum x1, blocking collectives, per_device(): lax.psum((gate_squared_columns, up_squared_columns), 'mp')  39.6 us
    psum x1, blocking collectives, per_device(): lax.psum(mag_gate_terms.astype(jnp.bfloat16), 'mp').astype(jnp.float32)  37.1 us
    unnamed x48, local copies, waits for them, and re-layouts  33 us
  transfers between devices with their start and end apart: 14, of which 8 were waited for; matrix products, arithmetic and copies ran while one was open for 20% of the time, Pallas kernels for 0%

profile of v1, /device:TPU:0, one launch (start us, length us, event | category | flops | bytes accessed | tf_op | source)
XLA Modules:
  0.0 649.2 jit_solution(14043339266614275368)
XLA Ops:
  7.2 9.0 %all_gather.18 = bf16[256,1024]{1,0:T(8,128)(2,1)S(1)} all-gather(bf16[64,1024]{1,0:T(8,128)(2,1)} %param.14), channel_id=1, replica_groups=mesh['dp'=4,'mp'=8] {'dp'}, dimensions={0}, use_global_device_ids=true | all-gather | bytes 655360 | tf_op jit(solution)/shard_map/all_gather | solution.py:94
  16.2 14.9 %multiply_reduce_fusion.2 = (f32[7168]{0:T(1024)S(1)}, f32[1024,7168]{1,0:T(8,128)}) fusion(bf16[1024,7168]{1,0:T(8,128)(2,1)} %param.15, bf16[1024,16]{0,1:T(8,128)(2,1)} %param.18, bf16[16,7168]{1,0:T(8,128)(2,1)} %param.19), kind=kOutput, calls=%fused_computation.3 | convolution fusion | flops 264233984 | bytes 44331008 | tf_op jit(solution)/shard_map/dot_general | solution.py:10
  31.2 18.4 %fusion.3 = bf16[256,7168]{0,1:T(8,128)(2,1)} fusion(bf16[256,1024]{1,0:T(8,128)(2,1)S(1)} %all_gather.18, f32[1024,7168]{1,0:T(8,128)} %get-tuple-element.36, bf16[1024,7168]{1,0:T(8,128)(2,1)} %param.15), kind=kOutput, calls=%fused_computation.12 | convolution fusion | flops 3781951488 | bytes 48234496 | tf_op jit(solution)/shard_map/dot_general | solution.py:10
  49.6 14.8 %multiply_reduce_fusion.1 = (f32[7168]{0:T(1024)S(1)}, f32[1024,7168]{1,0:T(8,128)}) fusion(bf16[1024,7168]{1,0:T(8,128)(2,1)} %param.16, bf16[1024,16]{0,1:T(8,128)(2,1)S(1)} %copy-done.7, bf16[16,7168]{1,0:T(8,128)(2,1)S(1)} %copy-done), kind=kOutput, calls=%fused_computation.2 | convolution fusion | flops 264233984 | bytes 44331008 | tf_op jit(solution)/shard_map/dot_general | solution.py:10
  64.4 18.4 %fusion.4 = bf16[256,7168]{0,1:T(8,128)(2,1)} fusion(bf16[256,1024]{1,0:T(8,128)(2,1)S(1)} %all_gather.18, f32[1024,7168]{1,0:T(8,128)} %get-tuple-element.34, bf16[1024,7168]{1,0:T(8,128)(2,1)} %param.16), kind=kOutput, calls=%fused_computation.13 | convolution fusion | flops 3781951488 | bytes 48234496 | tf_op jit(solution)/shard_map/dot_general | solution.py:10
  82.8 8.8 %pad_maximum_fusion = bf16[256,14336]{0,1:T(8,128)(2,1)} fusion(bf16[256,7168]{0,1:T(8,128)(2,1)} %fusion.4, bf16[256,7168]{0,1:T(8,128)(2,1)} %fusion.3), kind=kLoop, calls=%fused_computation.16 | loop fusion | flops 14680064 | bytes 14680064 | tf_op jit(solution)/shard_map/concatenate | solution.py:109
  91.6 10.0 %copy.54 = bf16[256,14336]{1,0:T(8,128)(2,1)} copy(bf16[256,14336]{0,1:T(8,128)(2,1)} %pad_maximum_fusion) | data formatting | bytes 14680064
  102.6 15.2 %multiply_reduce_fusion = (f32[1024]{0:T(1024)S(1)}, f32[7168,1024]{1,0:T(8,128)}) fusion(bf16[7168,1024]{1,0:T(8,128)(2,1)} %param.17, bf16[7168,16]{0,1:T(8,128)(2,1)S(1)} %copy-done.5, bf16[16,1024]{1,0:T(8,128)(2,1)S(1)} %copy-done.9), kind=kOutput, calls=%fused_computation | convolution fusion | flops 264240128 | bytes 44306432 | tf_op jit(solution)/shard_map/dot_general | solution.py:10
  117.7 7.1 %psum.100 = f32[1024]{0:T(1024)S(1)} all-reduce(f32[1024]{0:T(1024)S(1)} %get-tuple-element.31), channel_id=1, replica_groups=mesh['dp'=4,'mp'=8] {'dp'}, use_global_device_ids=true, to_apply=%region_7.0 | all-reduce | flops 1024 | bytes 8192 | tf_op jit(solution)/shard_map/psum | solution.py:87
  124.9 6.6 %all_gather.19 = bf16[256,1024]{1,0:T(8,128)(2,1)S(1)} all-gather(bf16[64,1024]{1,0:T(8,128)(2,1)S(1)} %fusion.22), channel_id=1, replica_groups=mesh['dp'=4,'mp'=8] {'dp'}, dimensions={0}, use_global_device_ids=true | all-gather | bytes 655360 | tf_op jit(solution)/shard_map/all_gather | solution.py:155
  131.5 18.7 %convolution_convert_fusion.2 = bf16[256,7168]{1,0:T(8,128)(2,1)} fusion(bf16[256,1024]{1,0:T(8,128)(2,1)S(1)} %all_gather.19, f32[7168,1024]{1,0:T(8,128)} %get-tuple-element.32, bf16[7168,1024]{1,0:T(8,128)(2,1)} %param.17), kind=kOutput, calls=%fused_computation.11 | convolution fusion | flops 3781951488 | bytes 48234496 | tf_op jit(solution)/shard_map/dot_general | solution.py:14
  150.3 39.6 %all-reduce = (f32[7168]{0:T(1024)S(1)}, f32[7168]{0:T(1024)S(1)}) all-reduce(f32[7168]{0:T(1024)S(1)} %get-tuple-element.33, f32[7168]{0:T(1024)S(1)} %get-tuple-element.35), channel_id=1, replica_groups=mesh['dp'=4,'mp'=8] {'mp'}, use_global_device_ids=true, to_apply=%region_4.0 | all-reduce | flops 14336 | bytes 114688 | tf_op jit(solution)/shard_map/psum | solution.py:84
  190.7 46.0 %reduce-scatter.13.cloned.1.call-done = bf16[32,14336]{1,0:T(8,128)(2,1)} async-done(((bf16[256,14336]{1,0:T(8,128)(2,1)}), bf16[32,14336]{1,0:T(8,128)(2,1)}) %reduce-scatter.13.cloned.1.call-update) | async-done | bytes 917520 | tf_op jit(solution)/shard_map/reduce_scatter | solution.py:108
  236.7 2.5 convert_element_type.113
  239.2 81.1 %reduce-scatter.15.cloned.1.call-done = bf16[32,7168]{1,0:T(8,128)(2,1)} async-done(((bf16[256,7168]{1,0:T(8,128)(2,1)}), bf16[32,7168]{1,0:T(8,128)(2,1)}) %reduce-scatter.15.cloned.1.call-update) | async-done | bytes 458768 | tf_op jit(solution)/shard_map/reduce_scatter | solution.py:167
  320.3 2.4 multiply_reduce_fusion.3
  322.8 37.1 %all-reduce.2 = (bf16[7168]{0:T(1024)(128)(2,1)}, bf16[7168]{0:T(1024)(128)(2,1)}, bf16[256,16]{0,1:T(8,128)(2,1)S(1)}, bf16[256,16]{0,1:T(8,128)(2,1)S(1)}, bf16[256,16]{0,1:T(8,128)(2,1)}) all-reduce(bf16[7168]{0:T(1024)(128)(2,1)S(1)} %get-tuple-element.12, ...), channel_id=1, replica_groups=mesh['dp'=4,'mp'=8] {'mp'}, use_global_device_ids=true, to_apply=%region_11.12 | all-reduce | flops 26624 | bytes 106496 | tf_op jit(solution)/shard_map/psum | solution.py:195
  362.5 19.9 %collective-permute-done = bf16[32,7168]{1,0:T(8,128)(2,1)S(1)} collective-permute-done((bf16[32,7168]{1,0:T(8,128)(2,1)S(1)}, bf16[32,7168]{1,0:T(8,128)(2,1)S(1)}, u32[]{:S(2)}, u32[]{:S(2)}) %collective-permute-start) | collective-permute-done | bytes 458784 | tf_op jit(solution)/shard_map/ppermute | solution.py:126
  382.5 17.2 %collective-permute-done.1 = bf16[32,7168]{1,0:T(8,128)(2,1)S(1)} collective-permute-done((bf16[32,7168]{1,0:T(8,128)(2,1)S(1)}, bf16[32,7168]{1,0:T(8,128)(2,1)S(1)}, u32[]{:S(2)}, u32[]{:S(2)}) %collective-permute-start.1) | collective-permute-done | bytes 458784 | tf_op jit(solution)/shard_map/ppermute | solution.py:126
  399.7 16.4 %collective-permute-done.2 = bf16[32,7168]{1,0:T(8,128)(2,1)S(1)} collective-permute-done((bf16[32,7168]{1,0:T(8,128)(2,1)S(1)}, bf16[32,7168]{1,0:T(8,128)(2,1)S(1)}, u32[]{:S(2)}, u32[]{:S(2)}) %collective-permute-start.2) | collective-permute-done | bytes 458784 | tf_op jit(solution)/shard_map/ppermute | solution.py:126
  416.9 14.8 %collective-permute-done.3 = bf16[32,7168]{1,0:T(8,128)(2,1)} collective-permute-done((bf16[32,7168]{1,0:T(8,128)(2,1)S(1)}, bf16[32,7168]{1,0:T(8,128)(2,1)}, u32[]{:S(2)}, u32[]{:S(2)}) %collective-permute-start.3) | collective-permute-done | bytes 458784 | tf_op jit(solution)/shard_map/ppermute | solution.py:126
  433.1 17.2 %collective-permute-done.4 = bf16[32,7168]{1,0:T(8,128)(2,1)} collective-permute-done((bf16[32,7168]{1,0:T(8,128)(2,1)}, bf16[32,7168]{1,0:T(8,128)(2,1)}, u32[]{:S(2)}, u32[]{:S(2)}) %collective-permute-start.4) | collective-permute-done | bytes 458784 | tf_op jit(solution)/shard_map/ppermute | solution.py:126
  452.2 10.6 %all-reduce.1 = (bf16[32,16]{0,1:T(8,128)(2,1)S(1)}, bf16[32,16]{0,1:T(8,128)(2,1)S(1)}) all-reduce(f32[32,16]{0,1:T(8,128)} %fusion.42, f32[32,16]{0,1:T(8,128)S(1)} %fusion.43), channel_id=1, replica_groups=mesh['dp'=4,'mp'=8] {'dp'}, use_global_device_ids=true, to_apply=%region_18.19 | all-reduce | flops 1024 | bytes 6144 | tf_op jit(solution)/shard_map/psum | solution.py:178
  462.8 31.3 %all-gather.1 = bf16[8,32,16]{1,2,0:T(8,128)(2,1)S(1)} all-gather(bf16[1,32,16]{1,2,0:T(8,128)(2,1)S(1)} %bitcast.52), channel_id=1, replica_groups=mesh['dp'=4,'mp'=8] {'mp'}, dimensions={0}, use_global_device_ids=true | all-gather | bytes 9216 | tf_op jit(solution)/shard_map/all_gather | solution.py:187
  494.2 31.4 %all-gather = bf16[8,32,16]{1,2,0:T(8,128)(2,1)S(1)} all-gather(bf16[1,32,16]{1,2,0:T(8,128)(2,1)S(1)} %bitcast.51), channel_id=1, replica_groups=mesh['dp'=4,'mp'=8] {'mp'}, dimensions={0}, use_global_device_ids=true | all-gather | bytes 9216 | tf_op jit(solution)/shard_map/all_gather | solution.py:186
  535.5 13.6 %collective-permute-done.6 = bf16[32,7168]{1,0:T(8,128)(2,1)} collective-permute-done((bf16[32,7168]{1,0:T(8,128)(2,1)}, bf16[32,7168]{1,0:T(8,128)(2,1)}, u32[]{:S(2)}, u32[]{:S(2)}) %collective-permute-start.6) | collective-permute-done | bytes 458784 | tf_op jit(solution)/shard_map/ppermute | solution.py:126
  570.4 17.7 %fusion.12 = bf16[256,1024]{1,0:T(8,128)(2,1)} fusion(bf16[512,7168]{1,0:T(8,128)(2,1)} %constant_dynamic-update-slice_fusion, s32[]{:T(128)S(6)} %select_n.18, f32[7168,1024]{1,0:T(8,128)} %get-tuple-element.32, bf16[7168,1024]{1,0:T(8,128)(2,1)} %param.17), kind=kOutput, calls=%fused_computation.25 | convolution fusion | flops 3780378624 | bytes 48234500 | tf_op jit(solution)/shard_map/dot_general | solution.py:10
  588.2 16.3 %fusion.38 = f32[256,1024]{1,0:T(8,128)S(1)} fusion(bf16[256,7168]{1,0:T(8,128)(2,1)} %all-gather.5.cloned.1.call-done, f32[1024,7168]{1,0:T(8,128)} %get-tuple-element.36, bf16[1024,7168]{1,0:T(8,128)(2,1)} %param.15), kind=kOutput, calls=%fused_computation.85 | convolution fusion | flops 3780116480 | bytes 48758784 | tf_op jit(solution)/shard_map/dot_general | solution.py:14
  604.5 17.4 %fusion.11 = bf16[256,1024]{1,0:T(8,128)(2,1)} fusion(f32[256,1024]{1,0:T(8,128)S(1)} %fusion.38, bf16[256,7168]{1,0:T(8,128)(2,1)} %all-gather.7.cloned.1.call-done, f32[1024,7168]{1,0:T(8,128)} %get-tuple-element.34, bf16[1024,7168]{1,0:T(8,128)(2,1)} %param.16), kind=kOutput, calls=%fused_computation.24 | convolution fusion | flops 3780640768 | bytes 49283072 | tf_op jit(solution)/shard_map/dot_general | solution.py:14
  622.0 3.1 fusion.15
  625.1 3.5 fusion.5
  630.2 10.7 %all-reduce.4 = (bf16[1024]{0:T(1024)(128)(2,1)S(1)}, bf16[256,16]{0,1:T(8,128)(2,1)S(1)}) all-reduce(bf16[1024]{0:T(1024)(128)(2,1)S(1)} %get-tuple-element.29, bf16[256,16]{0,1:T(8,128)(2,1)S(1)} %fusion.15), channel_id=1, replica_groups=mesh['dp'=4,'mp'=8] {'dp'}, use_global_device_ids=true, to_apply=%region_15.16 | all-reduce | flops 5120 | bytes 20480 | tf_op jit(solution)/shard_map/psum | solution.py:149
  (97 shorter events, 42.9 us)
Async XLA Ops:
  7.2 42.4 %copy-start = (bf16[16,7168]{1,0:T(8,128)(2,1)S(1)}, bf16[16,7168]{1,0:T(8,128)(2,1)}, u32[]{:S(2)}) copy-start(bf16[16,7168]{1,0:T(8,128)(2,1)} %param.21) | copy-start | bytes 688132
  7.2 229.5 %reduce-scatter.13.cloned.1.call-start = ((), (), s32[]{:S(2)}) async-start(), calls=%async_computation.8 | async-start | bytes 8257536 | tf_op jit(solution)/shard_map/reduce_scatter | solution.py:108
  31.2 18.4 %copy-start.7 = (bf16[1024,16]{0,1:T(8,128)(2,1)S(1)}, bf16[1024,16]{0,1:T(8,128)(2,1)}, u32[]{:S(2)}) copy-start(bf16[1024,16]{0,1:T(8,128)(2,1)} %param.20) | copy-start | bytes 98308
  101.6 0.9 copy-start.5
  101.6 0.9 copy-start.9
  101.7 23.2 %copy-start.14 = (f32[1024]{0:T(1024)S(1)}, f32[1024]{0:T(1024)}, u32[]{:S(2)}) copy-start(f32[1024]{0:T(1024)} %param.26) | copy-start | bytes 12292
  101.7 23.2 %copy-start.6 = (bf16[64,1024]{1,0:T(8,128)(2,1)S(1)}, bf16[64,1024]{1,0:T(8,128)(2,1)}, u32[]{:S(2)}) copy-start(bf16[64,1024]{1,0:T(8,128)(2,1)} %param.27) | copy-start | bytes 393220
  101.7 218.7 %reduce-scatter.15.cloned.1.call-start = ((), (), s32[]{:S(2)}) async-start(), calls=%async_computation.9 | async-start | bytes 4128768 | tf_op jit(solution)/shard_map/reduce_scatter | solution.py:167
  131.5 58.4 %copy-start.11 = (f32[7168]{0:T(1024)S(1)}, f32[7168]{0:T(1024)}, u32[]{:S(2)}) copy-start(f32[7168]{0:T(1024)} %param.24) | copy-start | bytes 86020
  131.5 58.4 %copy-start.12 = (f32[7168]{0:T(1024)S(1)}, f32[7168]{0:T(1024)}, u32[]{:S(2)}) copy-start(f32[7168]{0:T(1024)} %param.25) | copy-start | bytes 86020
  131.5 58.7 %copy-start.8 = (bf16[1024,16]{0,1:T(8,128)(2,1)S(1)}, bf16[1024,16]{0,1:T(8,128)(2,1)}, u32[]{:S(2)}) copy-start(bf16[1024,16]{0,1:T(8,128)(2,1)} %param.18) | copy-start | bytes 98308
  150.3 381.7 %all-reduce.7.cloned.1.call-start = ((), (), s32[]{:S(2)}) async-start(), calls=%async_computation.10 | async-start | bytes 917504 | tf_op jit(solution)/shard_map/psum | solution.py:197
  189.9 272.9 %copy-start.10 = (f32[7168]{0:T(1024)}, f32[7168]{0:T(1024)S(1)}, u32[]{:S(2)}) copy-start(f32[7168]{0:T(1024)S(1)} %get-tuple-element.14) | copy-start | bytes 86020
  322.7 109.0 %copy-start.1 = (bf16[32,7168]{1,0:T(8,128)(2,1)}, bf16[32,7168]{1,0:T(8,128)(2,1)S(1)}, u32[]{:S(2)}) copy-start(bf16[32,7168]{1,0:T(8,128)(2,1)S(1)} %get-tuple-element.27) | copy-start | bytes 1376260
  322.8 39.1 %copy-start.2 = (bf16[32,7168]{1,0:T(8,128)(2,1)}, bf16[32,7168]{1,0:T(8,128)(2,1)S(1)}, u32[]{:S(2)}) copy-start(bf16[32,7168]{1,0:T(8,128)(2,1)S(1)} %multiply_convert_fusion.1) | copy-start | bytes 1376260
  361.9 226.3 %all-gather.5.cloned.1.call-start = ((), (), s32[]{:S(2)}) async-start(), calls=%async_computation.5 | async-start | bytes 4128768 | tf_op jit(solution)/shard_map/all_gather | solution.py:205
  362.4 242.1 %all-gather.7.cloned.1.call-start = ((), (), s32[]{:S(2)}) async-start(), calls=%async_computation.6 | async-start | bytes 4128768 | tf_op jit(solution)/shard_map/all_gather | solution.py:206
  362.5 20.0 %collective-permute-start = (bf16[32,7168]{1,0:T(8,128)(2,1)S(1)}, bf16[32,7168]{1,0:T(8,128)(2,1)S(1)}, u32[]{:S(2)}, u32[]{:S(2)}) collective-permute-start(bf16[32,7168]{1,0:T(8,128)(2,1)S(1)} %get-tuple-element.28), channel_id=1, source_target_pairs={{0,1},{1,2},{2,3},{3,4},{4,5},{5,6},{6,7},{7,0},{8,9},{9,10},{10,1... | collective-permute-start | bytes 1376264 | tf_op jit(solution)/shard_map/ppermute | solution.py:126
  382.5 17.2 %collective-permute-start.1 = (bf16[32,7168]{1,0:T(8,128)(2,1)S(1)}, bf16[32,7168]{1,0:T(8,128)(2,1)S(1)}, u32[]{:S(2)}, u32[]{:S(2)}) collective-permute-start(bf16[32,7168]{1,0:T(8,128)(2,1)S(1)} %collective-permute-done), channel_id=1, source_target_pairs={{0,1},{1,2},{2,3},{3,4},{4,5},{5,6},{6,7},{7,0},{8,9},{9,10},{10,1... | collective-permute-start | bytes 1376264 | tf_op jit(solution)/shard_map/ppermute | solution.py:126
  399.7 16.4 %collective-permute-start.2 = (bf16[32,7168]{1,0:T(8,128)(2,1)S(1)}, bf16[32,7168]{1,0:T(8,128)(2,1)S(1)}, u32[]{:S(2)}, u32[]{:S(2)}) collective-permute-start(bf16[32,7168]{1,0:T(8,128)(2,1)S(1)} %collective-permute-done.1), channel_id=1, source_target_pairs={{0,1},{1,2},{2,3},{3,4},{4,5},{5,6},{6,7},{7,0},{8,9},{9,10},{10,1... | collective-permute-start | bytes 1376264 | tf_op jit(solution)/shard_map/ppermute | solution.py:126
  416.1 0.8 copy-start.3
  416.9 14.8 %collective-permute-start.3 = (bf16[32,7168]{1,0:T(8,128)(2,1)S(1)}, bf16[32,7168]{1,0:T(8,128)(2,1)}, u32[]{:S(2)}, u32[]{:S(2)}) collective-permute-start(bf16[32,7168]{1,0:T(8,128)(2,1)S(1)} %collective-permute-done.2), channel_id=1, source_target_pairs={{0,1},{1,2},{2,3},{3,4},{4,5},{5,6},{6,7},{7,0},{8,9},{9,10},{10,1... | collective-permute-start | bytes 1376264 | tf_op jit(solution)/shard_map/ppermute | solution.py:126
  431.7 18.6 %collective-permute-start.4 = (bf16[32,7168]{1,0:T(8,128)(2,1)}, bf16[32,7168]{1,0:T(8,128)(2,1)}, u32[]{:S(2)}, u32[]{:S(2)}) collective-permute-start(bf16[32,7168]{1,0:T(8,128)(2,1)} %collective-permute-done.3), channel_id=1, source_target_pairs={{0,1},{1,2},{2,3},{3,4},{4,5},{5,6},{6,7},{7,0},{8,9},{9,10},{10,1... | collective-permute-start | bytes 1376264 | tf_op jit(solution)/shard_map/ppermute | solution.py:126
  431.7 124.9 %copy-start.4 = (bf16[32,7168]{1,0:T(8,128)(2,1)S(1)}, bf16[32,7168]{1,0:T(8,128)(2,1)}, u32[]{:S(2)}) copy-start(bf16[32,7168]{1,0:T(8,128)(2,1)} %copy-done.3) | copy-start | bytes 1376260
  431.8 196.8 %reduce-scatter.9.cloned.1.call-start = ((), (), s32[]{:S(2)}) async-start(), calls=%async_computation.4 | async-start | bytes 655360 | tf_op jit(solution)/shard_map/reduce_scatter | solution.py:136
  450.3 77.6 %collective-permute-start.5 = (bf16[32,7168]{1,0:T(8,128)(2,1)}, bf16[32,7168]{1,0:T(8,128)(2,1)}, u32[]{:S(2)}, u32[]{:S(2)}) collective-permute-start(bf16[32,7168]{1,0:T(8,128)(2,1)} %collective-permute-done.4), channel_id=1, source_target_pairs={{0,1},{1,2},{2,3},{3,4},{4,5},{5,6},{6,7},{7,0},{8,9},{9,10},{10,1... | collective-permute-start | bytes 1376264 | tf_op jit(solution)/shard_map/ppermute | solution.py:126
  527.9 21.2 %collective-permute-start.6 = (bf16[32,7168]{1,0:T(8,128)(2,1)}, bf16[32,7168]{1,0:T(8,128)(2,1)}, u32[]{:S(2)}, u32[]{:S(2)}) collective-permute-start(bf16[32,7168]{1,0:T(8,128)(2,1)} %collective-permute-done.5), channel_id=1, source_target_pairs={{0,1},{1,2},{2,3},{3,4},{4,5},{5,6},{6,7},{7,0},{8,9},{9,10},{10,1... | collective-permute-start | bytes 1376264 | tf_op jit(solution)/shard_map/ppermute | solution.py:126
  588.1 54.3 %reduce-scatter.11.cloned.1.call-start = ((), (), s32[]{:S(2)}) async-start(), calls=%async_computation.7 | async-start | bytes 655360 | tf_op jit(solution)/shard_map/reduce_scatter | solution.py:212
  604.5 20.6 %copy-start.13 = (bf16[256,16]{0,1:T(8,128)(2,1)S(1)}, bf16[256,16]{0,1:T(8,128)(2,1)}, u32[]{:S(2)}) copy-start(bf16[256,16]{0,1:T(8,128)(2,1)} %get-tuple-element.21) | copy-start | bytes 24580
Sparse Core Ops, SparseCore 0:
  101.8 134.8 reduce-scatter.12
  240.3 79.9 reduce-scatter.14
  362.0 81.2 all-reduce.6
  445.4 69.4 all-gather.4
  516.9 69.5 all-gather.6
  588.8 20.3 reduce-scatter.8
  622.1 19.0 reduce-scatter.10
